TPU v7x, 32 devices: a whole 2x2x4 slice. The times are simulated.
32 devices in a mesh: member: 4 (over z), py: 4 (over x, core), pz: 2 (over y).
Axes of the slice: x: 2, y: 2, z: 4, core: 2. Of those that a mesh axis runs over, the one named last changes fastest.
Arguments:
- velocity_hat: float32 [8, 3, 96, 36864], P('member', None, None, ('py', 'pz')), parts along dimension 0, may hold values from -448 to 448
- time_step: float32 [4], P('member'), parts along dimension 0, may hold values from 0.003 to 0.006
- power: float32 [4], P('member'), parts along dimension 0, may hold values from 20 to 80
- cutoffs: int32 [12], P('member'), parts along dimension 0, may hold values from 48 to 64, as said below
Outputs:
- velocity_next: float32 [8, 3, 96, 36864], P('member', None, None, ('py', 'pz')), parts along dimension 0
- cfl_number: float32 [4], P('member'), parts along dimension 0
- energy: float32 [4], P('member'), parts along dimension 0
There are 4 independent parts, one for each index of `member`. A program takes and returns all parts, laid end to end along the dimension named above; each array names one. Nothing has to cross between parts.
Inputs may be any that keep to these rules, and one draw needn't show every extreme that they name: `cutoffs`: in every draw one of the three equals 64.
All inputs are finite; a program needn't handle non-finite values.
Results may differ from a plain program's by a relative error of at most 0.0002.
Values sent between devices are 32-bit elements; how exact they have to be, the bound alone decides.
A program may use at most 256 MiB of HBM per device.

v0:
```python
import math

import jax
import jax.numpy as jnp
from jax import lax
from jax.sharding import PartitionSpec as P

viscosity = 0.004
keep_share = (0.0, 0.75, 1.0 / 3.0)
highest = lax.Precision.HIGH


def phases(length, row_count, col_count, handed):
    row_index = lax.broadcasted_iota(jnp.int32, (row_count, col_count), 0)
    col_index = lax.broadcasted_iota(jnp.int32, (row_count, col_count), 1)
    windings = row_index * col_index % length
    angles = windings.astype(jnp.float32) * (2.0 * math.pi / length)
    return (jnp.cos(angles), handed * jnp.sin(angles))


def complex_table(length, handed):
    cosine, sine_part = phases(length, length, length, handed)
    return jnp.stack([jnp.stack([cosine, sine_part]), jnp.stack([-sine_part, cosine])])


def depth_tables(length):
    factor = float(length) ** (-1.5)
    cosine, sine_part = phases(length, length // 2, length, 1.0)
    weight = jnp.where(lax.broadcasted_iota(jnp.int32, (length // 2, 1), 0) == 0, 1.0, 2.0)
    backward = jnp.stack([weight * cosine, -weight * sine_part]) * factor
    onward = jnp.stack([cosine.T, -sine_part.T], axis=1) * factor
    return (backward, onward)


def slab_spread(fields, group_size, slab_width, table):
    points = table.shape[-1]
    return jnp.einsum(
        "rmlk,rskgx->gsxlm",
        fields,
        table.reshape(2, 2, points, group_size, slab_width),
        precision=highest,
    )


def slab_rows(received, group_size, cross_part, table, components):
    points = table.shape[-1]
    strips = jnp.einsum(
        "grxlm,rsgly->sxmy",
        received,
        table.reshape(2, 2, group_size, cross_part, points),
        precision=highest,
    )
    return strips.reshape(2, strips.shape[1], components, -1, points)


def slab_planes(physical, group_size, cross_part, onward_cut, table):
    components, slab_width, points = (physical.shape[0], physical.shape[1], physical.shape[3])
    depth_part = onward_cut.shape[2]
    planes = jnp.einsum("cxyz,zrj->rxcjy", physical, onward_cut, precision=highest)
    return jnp.einsum(
        "rxmy,rsygl->gsxlm",
        planes.reshape(2, slab_width, components * depth_part, points),
        table.reshape(2, 2, points, group_size, cross_part),
        precision=highest,
    )


def slab_close(received, group_size, slab_width, table):
    points = table.shape[-1]
    return jnp.einsum(
        "gsxlm,srgxk->rmlk",
        received,
        table.reshape(2, 2, group_size, slab_width, points),
        precision=highest,
    )


def turned(field):
    return jnp.stack([-field[1], field[0]])


def on_device(velocity_hat, time_step, power, cutoffs):
    count_y = lax.axis_size("py")
    count_z = lax.axis_size("pz")
    group_size = count_y * count_z
    half_depth = velocity_hat.shape[2]
    points = 2 * half_depth
    cross_part = velocity_hat.shape[3] // points
    flat_width = velocity_hat.shape[3]
    slab_width = points // group_size
    depth_keep = min(half_depth, (points // 3 + 8) // 8 * 8)
    inverse_table = complex_table(points, 1.0)
    forward_table = complex_table(points, -1.0)
    backward, onward = depth_tables(points)
    backward_cut = backward[:, :depth_keep]
    onward_cut = onward[:, :, :depth_keep]
    depth_wave = lax.broadcasted_iota(jnp.int32, (half_depth, 1, 1), 0)
    cross_index = lax.axis_index(("py", "pz")) * cross_part + lax.broadcasted_iota(
        jnp.int32, (1, cross_part, 1), 1
    )
    cross_wave = jnp.where(cross_index < points // 2, cross_index, cross_index - points)
    along_index = lax.broadcasted_iota(jnp.int32, (1, 1, points), 2)
    along_wave = jnp.where(along_index < points // 2, along_index, along_index - points)
    keep_mask = (
        (jnp.abs(along_wave) <= cutoffs[0])
        & (jnp.abs(cross_wave) <= cutoffs[1])
        & (depth_wave <= cutoffs[2])
    ).astype(jnp.float32)
    waves = (
        along_wave.astype(jnp.float32),
        cross_wave.astype(jnp.float32),
        depth_wave.astype(jnp.float32),
    )
    wave_square = waves[0] * waves[0] + waves[1] * waves[1] + waves[2] * waves[2]
    inverse_square = 1.0 / jnp.maximum(wave_square, 1.0)

    def project(field):
        normal_part = waves[0] * field[:, 0] + waves[1] * field[:, 1] + waves[2] * field[:, 2]
        return jnp.stack(
            [
                keep_mask
                * (field[:, axis_index] - waves[axis_index] * normal_part * inverse_square)
                for axis_index in range(3)
            ],
            axis=1,
        )

    step_size = time_step[0]
    current = velocity_hat.reshape(2, 3, half_depth, cross_part, points)
    solenoidal = project(current)
    kept = solenoidal[:, :, :depth_keep]
    fields = jnp.concatenate(
        [
            kept,
            turned(waves[0] * kept[:, 2])[:, None],
            turned(waves[0] * kept[:, 1] - waves[1] * kept[:, 0])[:, None],
        ],
        axis=1,
    ).reshape(2, 5 * depth_keep, cross_part, points)
    received = lax.all_to_all(
        slab_spread(fields, group_size, slab_width, inverse_table),
        ("py", "pz"),
        split_axis=0,
        concat_axis=0,
        tiled=True,
    )
    row_index = lax.broadcasted_iota(jnp.int32, (points, 1), 0)
    row_wave = jnp.where(row_index < points // 2, row_index, row_index - points)
    row_wave = row_wave.astype(jnp.float32)
    slope_table = jnp.stack(
        [-row_wave * inverse_table[:, 1], row_wave * inverse_table[:, 0]], axis=1
    )
    rows = slab_rows(received, group_size, cross_part, inverse_table, 5)
    slope = slab_rows(
        received[..., 2 * depth_keep : 3 * depth_keep], group_size, cross_part, slope_table, 1
    )
    kz = lax.broadcasted_iota(jnp.int32, (depth_keep, 1), 0).astype(jnp.float32)
    strips = jnp.stack(
        [
            rows[:, :, 0],
            rows[:, :, 1],
            rows[:, :, 2],
            slope[:, :, 0] - turned(kz * rows[:, :, 1]),
            turned(kz * rows[:, :, 0]) - rows[:, :, 3],
            rows[:, :, 4],
        ],
        axis=2,
    )
    physical = jnp.einsum("sxcjy,sjz->cxyz", strips, backward_cut, precision=highest)
    velocity = physical[:3]
    vorticity = physical[3:]
    nonlinear = jnp.stack(
        [
            velocity[1] * vorticity[2] - velocity[2] * vorticity[1],
            velocity[2] * vorticity[0] - velocity[0] * vorticity[2],
            velocity[0] * vorticity[1] - velocity[1] * vorticity[0],
        ]
    )
    local_fastest = jnp.max(jnp.abs(velocity[0]) + jnp.abs(velocity[1]) + jnp.abs(velocity[2]))
    local_squares = jnp.sum(velocity * velocity)
    fastest = lax.pmax(local_fastest, ("py", "pz"))
    summed = lax.psum(local_squares, ("py", "pz"))
    energy = 0.5 * summed / float(points**3)
    layers = slab_planes(nonlinear, group_size, cross_part, onward_cut, forward_table)
    spectra = slab_close(
        lax.all_to_all(layers, ("py", "pz"), split_axis=0, concat_axis=0, tiled=True),
        group_size,
        slab_width,
        forward_table,
    ).reshape(2, 3, depth_keep, cross_part, points)
    spectra = jnp.concatenate(
        [spectra, jnp.zeros((2, 3, half_depth - depth_keep, cross_part, points), jnp.float32)],
        axis=2,
    )
    forced = project(spectra)
    forcing = power[0] / jnp.maximum(2.0 * energy, 0.5)
    update = solenoidal + step_size * (
        forced + forcing * solenoidal - viscosity * wave_square * solenoidal
    )
    keep_weight = keep_share[0]
    current = keep_weight * solenoidal + (1.0 - keep_weight) * update
    cfl_values = [step_size * fastest * points / (2.0 * math.pi)]
    energy_values = [energy]
    velocity_next = current.reshape(2, 3, half_depth, flat_width)
    return (velocity_next, jnp.stack(cfl_values), jnp.stack(energy_values))


def solution(mesh):
    return jax.shard_map(
        on_device,
        mesh=mesh,
        in_specs=(P("member", None, None, ("py", "pz")), P("member"), P("member"), P("member")),
        out_specs=(P("member", None, None, ("py", "pz")), P("member"), P("member")),
        check_vma=False,
    )
```

profile of v0, /device:TPU:0, one launch (start us, length us, event | category | flops | bytes accessed | tf_op | source)
XLA Modules:
  0.0 595.8 jit_solution(1255996920480460246)
XLA Ops:
  0.8 1.4 fusion.147
  2.1 0.6 iota_compare_fusion
  2.8 0.7 abs_compare_fusion.1
  3.4 0.7 abs_compare_fusion
  4.1 1.7 broadcast_multiply_fusion
  5.8 9.4 %copy.67 = f32[2,3,96,4608]{3,2,0,1:T(8,128)} copy(f32[2,3,96,4608]{3,2,1,0:T(8,128)} %param.4) | data formatting | bytes 21233664 | tf_op args[0]
  15.2 13.5 %reshape.541 = f32[2,3,96,24,192]{4,3,2,0,1:T(8,128)} reshape(f32[2,3,96,4608]{3,2,0,1:T(8,128)} %copy.67) | data formatting | bytes 21233664 | tf_op jit(solution)/shard_map/reshape | solution.py:129
  28.7 0.1 broadcast_and_fusion
  28.9 0.4 maximum_divide_fusion
  29.3 0.2 copy-done.12
  29.5 0.2 and_convert_fusion
  29.8 9.6 %fusion.43 = (f32[2,1,96,24,192]{4,3,2,1,0:T(8,128)S(1)}, f32[2,1,96,24,192]{4,3,2,0,1:T(8,128)}) fusion(f32[2,3,96,24,192]{4,3,2,0,1:T(8,128)} %reshape.541, f32[96,24,192]{2,1,0:T(8,128)S(1)} %maximum_divide_fusion, f32[192]{0:T(256)S(1)} %fusion.130, f32[96,24,192]{2,1,0:T(8,128)S(1)} %and_convert_fusion, f32[96]{0:T(128)S(1)} %iota_convert_fusion.1, ...), kind=kLoop, calls=%fused_computation.57 | loop fusion | flops 7962624 | bytes 21234912 | tf_op jit(solution)/shard_map/mul | solution.py:121
  39.4 1.1 slice-done.1
  40.6 2.8 slice-done.2
  43.3 0.4 slice-done.3
  43.8 6.0 %bitcast_multiply_fusion.3 = (f32[2,1,96,24,192]{4,3,2,0,1:T(8,128)}, f32[2,1,96,24,192]{4,3,2,0,1:T(8,128)S(1)}) fusion(f32[2,1,96,24,192]{4,3,2,0,1:T(8,128)} %get-tuple-element.6, f32[2,3,96,24,192]{4,3,2,0,1:T(8,128)S(1)} %bitcast.254, f32[96,24,192]{2,1,0:T(8,128)} %copy-done.3, f32[24]{0:T(128)S(1)} %fusion.133, f32[96,24,192]{2,1,0:T(8,128)} %copy-done.5, ...), kind=kLoop, calls=%fused_computation.37 | loop fusion | flops 7077888 | bytes 21234144 | tf_op jit(solution)/shard_map/mul | solution.py:121
  49.8 6.2 %fusion.53 = (f32[2,72,24,192]{3,2,1,0:T(8,128)S(1)}, f32[2,72,24,192]{3,2,1,0:T(8,128)}) fusion(f32[2,1,96,24,192]{4,3,2,0,1:T(8,128)S(1)} %get-tuple-element.12, f32[192]{0:T(256)S(1)} %fusion.130, f32[2,1,96,24,192]{4,3,2,1,0:T(8,128)S(1)} %get-tuple-element.5, f32[24]{0:T(128)S(1)} %fusion.133, f32[2,1,96,24,192]{4,3,2,0,1:T(8,128)} %get-tuple-element.11), kind=kLoop, calls=%fused_computation.78 | loop fusion | flops 2654208 | bytes 13271904 | tf_op jit(solution)/shard_map/mul | solution.py:135
  56.0 2.7 slice_negate_fusion.2
  58.7 0.2 maximum_bitcast_fusion.2
  58.9 2.0 maximum_bitcast_fusion.1
  61.0 4.7 fusion.9
  65.7 2.2 copy.81
  67.9 16.5 %fusion.30 = f32[8,2,24,24,360]{4,2,3,0,1:T(8,128)} fusion(f32[2,360,24,192,1,1]{3,2,1,0,5,4:T(8,128)S(1)} %bitcast.262, f32[1,1,192,8,24]{2,4,0,3,1:T(8,128)S(1)} %get-tuple-element.38, f32[1,1,192,8,24]{2,4,0,3,1:T(8,128)S(1)} %get-tuple-element.36, f32[1,1,192,8,24]{2,4,0,3,1:T(8,128)S(1)} %get-tuple-element.37), kind=kOutput, calls=%fused_computation.41 | convolution fusion | flops 7644561408 | bytes 26984448 | tf_op jit(solution)/shard_map/rmlk,rskgx->gsxlm/dot_general | solution.py:37
  84.3 11.4 %copy.83 = f32[8,2,24,24,360]{4,2,3,1,0:T(8,128)} copy(f32[8,2,24,24,360]{4,2,3,0,1:T(8,128)} %fusion.30) | data formatting | bytes 26542080 | tf_op jit(solution)/shard_map/rmlk,rskgx->gsxlm/transpose | solution.py:37
  95.7 5.7 all-to-all-start
  101.5 0.8 fusion.125
  102.3 1.1 sine_negate_fusion
  103.4 0.8 fusion.91
  104.3 1.1 sine_multiply_fusion
  105.4 1.0 fusion.81
  106.4 1.7 broadcast_multiply_fusion.1
  108.1 149.1 %all-to-all-done = f32[8,2,24,24,360]{4,2,3,1,0:T(8,128)} async-done(((f32[8,2,24,24,360]{4,2,3,1,0:T(8,128)}), f32[8,2,24,24,360]{4,2,3,1,0:T(8,128)}, u32[]{:S(2)}, u32[]{:S(2)}) %all-to-all-start) | async-done | bytes 13271072 | tf_op jit(solution)/shard_map/all_to_all | solution.py:140
  257.1 19.2 %fusion.27 = f32[2,24,360,192]{2,3,1,0:T(8,128)} fusion(f32[1,1,8,24,192]{4,3,0,2,1:T(8,128)S(1)} %get-tuple-element.33, f32[1,1,8,24,192]{4,3,0,2,1:T(8,128)S(1)} %get-tuple-element.31, f32[1,1,8,24,192]{4,3,0,2,1:T(8,128)S(1)} %get-tuple-element.32, f32[8,2,24,24,360]{4,2,3,1,0:T(8,128)} %all-to-all-done), kind=kOutput, calls=%fused_computation.40 | convolution fusion | flops 7644561408 | bytes 26984448 | tf_op jit(solution)/shard_map/grxlm,rsgly->sxmy/dot_general | solution.py:47
  276.3 16.9 %copy.85 = f32[2,24,360,192]{3,2,1,0:T(8,128)} copy(f32[2,24,360,192]{2,3,1,0:T(8,128)} %fusion.27) | data formatting | bytes 26542080 | tf_op jit(solution)/shard_map/grxlm,rsgly->sxmy/transpose | solution.py:47
  293.3 3.7 fusion.49
  297.0 0.2 slice_negate_fusion.1
  297.2 2.0 fusion.58
  299.3 12.8 %copy.84 = f32[8,2,24,24,360]{4,3,1,0,2:T(8,128)} copy(f32[8,2,24,24,360]{4,2,3,1,0:T(8,128)} %all-to-all-done) | data formatting | bytes 26542080 | tf_op jit(solution)/shard_map/all_to_all | solution.py:140
  312.1 7.6 %fusion.54 = f32[2,24,1,72,192]{4,3,1,0,2:T(8,128)S(1)} fusion(f32[1,24,72,192]{3,2,1,0:T(8,128)S(1)} %get-tuple-element.18, f32[1,24,72,192]{3,2,1,0:T(8,128)S(1)} %get-tuple-element.17, f32[8,2,24,24,360]{4,3,1,0,2:T(8,128)} %copy.84, f32[2,1,8,24,192]{4,3,2,0,1:T(8,128)} %bitcast.271, f32[2,1,8,24,192]{4,3,2,0,1:T(8,128)} %bitcast.270), kind=kOutput, calls=%fused_computation.82 | convolution fusion | flops 1530298368 | bytes 10813440 | tf_op jit(solution)/shard_map/grxlm,rsgly->sxmy/dot_general | solution.py:47
  319.7 21.9 %fusion.17 = f32[6,24,192,192]{2,3,0,1:T(8,128)} fusion(f32[1,96,192]{2,1,0:T(8,128)S(1)} %copy-done.22, f32[1,96,192]{2,1,0:T(8,128)S(1)} %copy-done.23, f32[2,24,1,72,192]{4,3,1,0,2:T(8,128)S(1)} %fusion.54, f32[2,24,5,72,192]{4,3,2,1,0:T(8,128)} %bitcast.261, f32[1,24,1,72,192]{4,3,1,2,0:T(8,128)S(1)} %copy-done.9, f32[1,24,1,72,192]{4,3,1,2,0:T(8,128)S(1)} %copy-done.8), kind=kOutput, calls=%fused_computation.24 | convolution fusion | flops 4599797760 | bytes 39960576 | tf_op jit(solution)/shard_map/sxcjy,sjz->cxyz/dot_general | solution.py:169
  341.5 17.2 %add_reduce_fusion = (f32[]{:T(128)}, f32[1,24,192,192]{2,3,0,1:T(8,128)}, f32[1,24,192,192]{2,3,0,1:T(8,128)}, f32[1,24,192,192]{2,3,0,1:T(8,128)}) fusion(f32[6,24,192,192]{2,3,0,1:T(8,128)} %fusion.17), kind=kLoop, calls=%fused_computation.59 | loop fusion | flops 13271039 | bytes 31850500 | tf_op jit(solution)/shard_map/reduce_max | solution.py:179
  358.7 8.2 %fusion.44 = f32[2,24,3,72,192]{4,3,1,2,0:T(8,128)S(1)} fusion(f32[192,1,96]{0,2,1:T(8,128)S(1)} %copy-done.10, f32[192,1,96]{0,2,1:T(8,128)S(1)} %copy-done.11, f32[1,24,192,192]{2,3,0,1:T(8,128)} %get-tuple-element.10, f32[1,24,192,192]{2,3,0,1:T(8,128)} %get-tuple-element.8, f32[1,24,192,192]{2,3,0,1:T(8,128)} %get-tuple-element.9), kind=kOutput, calls=%fused_computation.65 | convolution fusion | flops 2298599424 | bytes 18726912 | tf_op jit(solution)/shard_map/cxyz,zrj->rxcjy/dot_general | solution.py:59
  367.0 4.9 copy.98
  371.8 10.6 %convolution_bitcast_fusion = f32[8,2,24,24,216]{4,3,2,0,1:T(8,128)S(1)} fusion(f32[2,24,216,192,1,1]{3,2,1,0,5,4:T(8,128)} %bitcast.269, f32[1,1,192,8,24]{2,4,0,3,1:T(8,128)S(1)} %copy-done.17, f32[1,1,192,8,24]{2,4,0,3,1:T(8,128)S(1)} %copy-done.15, f32[1,1,192,8,24]{2,4,0,3,1:T(8,128)S(1)} %copy-done.14), kind=kOutput, calls=%fused_computation.84 | convolution fusion | flops 4586913792 | bytes 16367616 | tf_op jit(solution)/shard_map/rxmy,rsygl->gsxlm/dot_general | solution.py:60
  382.5 6.6 %copy.100 = f32[8,2,24,24,216]{4,2,1,3,0:T(8,128)} copy(f32[8,2,24,24,216]{4,3,2,0,1:T(8,128)S(1)} %convolution_bitcast_fusion) | data formatting | bytes 15925248 | tf_op jit(solution)/shard_map/rxmy,rsygl->gsxlm/transpose | solution.py:60
  389.0 5.5 all-to-all-start.1
  394.5 0.1 add.334
  394.6 5.5 stack.138
  400.1 5.5 stack.139
  405.6 5.5 stack.137
  411.8 1.5 add_multiply_fusion
  413.3 9.3 %fusion.12 = f32[]{:T(128)} fusion(f32[6,24,192,192]{2,3,0,1:T(8,128)} %fusion.17), kind=kLoop, calls=%fused_computation.18 | loop fusion | flops 5308415 | bytes 10616836 | tf_op jit(solution)/shard_map/reduce_sum | solution.py:180
  423.3 83.7 %psum.7 = f32[]{:T(128)} all-reduce(f32[]{:T(128)} %fusion.12), channel_id=1, replica_groups=mesh['member'=4,'py'=4,'pz'=2] {'py','pz'}, use_global_device_ids=true, to_apply=%region_1.2 | all-reduce | flops 1 | bytes 8 | tf_op jit(solution)/shard_map/psum | solution.py:182
  506.9 14.3 %pmax.7 = f32[]{:T(128)} all-reduce(f32[]{:T(128)} %get-tuple-element.7), channel_id=1, replica_groups=mesh['member'=4,'py'=4,'pz'=2] {'py','pz'}, use_global_device_ids=true, to_apply=%region_3.4 | all-reduce | flops 1 | bytes 8 | tf_op jit(solution)/shard_map/pmax | solution.py:181
  523.2 12.9 %fusion.55 = f32[2,216,24,192]{1,3,2,0:T(8,128)} fusion(f32[8,2,24,24,216]{4,2,1,3,0:T(8,128)} %all-to-all-done.1, f32[1,1,8,24,192]{4,3,0,2,1:T(8,128)S(1)} %copy-done.21, f32[1,1,8,24,192]{4,3,0,2,1:T(8,128)S(1)} %copy-done.19, f32[1,1,8,24,192]{4,3,0,2,1:T(8,128)S(1)} %copy-done.18), kind=kOutput, calls=%fused_computation.83 | convolution fusion | flops 4586913792 | bytes 16367616 | tf_op jit(solution)/shard_map/gsxlm,srgxk->rmlk/dot_general | solution.py:70
  536.0 12.4 %copy.102 = f32[2,216,24,192]{3,2,1,0:T(8,128)} copy(f32[2,216,24,192]{1,3,2,0:T(8,128)} %fusion.55) | data formatting | bytes 15925248 | tf_op jit(solution)/shard_map/gsxlm,srgxk->rmlk/transpose | solution.py:70
  548.5 9.1 %subtract_multiply_fusion.1 = (f32[2,1,96,24,192]{4,3,2,1,0:T(8,128)}, f32[2,1,96,24,192]{4,3,2,1,0:T(8,128)S(1)}) fusion(f32[2,3,72,24,192]{4,3,2,1,0:T(8,128)} %bitcast.255, f32[96,24,192]{2,1,0:T(8,128)S(1)} %copy-done.4, f32[192]{0:T(256)S(1)} %copy-done.25, f32[96,24,192]{2,1,0:T(8,128)} %copy-done.5, f32[96]{0:T(128)S(1)} %copy-done.29, ...), kind=kLoop, calls=%fused_computation.61 | loop fusion | flops 7962624 | bytes 18580704 | tf_op jit(solution)/shard_map/mul | solution.py:121
  557.6 1.5 copy-done
  559.1 0.7 copy-done.6
  559.8 4.6 subtract_multiply_fusion
  564.4 5.5 stack.173
  569.9 5.5 stack.174
  575.4 5.7 stack.175
  581.2 12.0 %fusion.23 = f32[2,3,96,4608]{3,2,1,0:T(8,128)} fusion(f32[2,1,96,4608]{3,2,1,0:T(8,128)} %bitcast.268, f32[2,1,96,4608]{3,2,1,0:T(8,128)} %bitcast.267, f32[2,1,96,4608]{3,2,1,0:T(8,128)} %bitcast.266, f32[2,1,96,4608]{3,2,1,0:T(8,128)} %bitcast.264, f32[2,1,96,4608]{3,2,1,0:T(8,128)S(1)} %bitcast.263, f32[2,1,96,4608]{3,2,1,0:T(8,128)} %bitcast.265, ...), kind=kLoop, calls=%fused_computation.30 | loop fusion | flops 31850496 | bytes 33619976 | tf_op jit(solution)/shard_map/add | solution.py:201
  (86 shorter events, 0.3 us)
Async XLA Ops:
  0.6 38.8 %copy-start.28 = (f32[96]{0:T(128)}, f32[96]{0:T(128)S(1)}, u32[]{:S(2)}) copy-start(f32[96]{0:T(128)S(1)} %iota_convert_fusion.1) | copy-start | bytes 1156
  0.7 28.2 %copy-start.30 = (f32[96]{0:T(128)}, f32[96]{0:T(128)S(1)}, u32[]{:S(2)}) copy-start(f32[96]{0:T(128)S(1)} %fusion.134) | copy-start | bytes 1156
  0.7 49.1 %copy-start.26 = (f32[24]{0:T(128)}, f32[24]{0:T(128)S(1)}, u32[]{:S(2)}) copy-start(f32[24]{0:T(128)S(1)} %fusion.133) | copy-start | bytes 292
  0.7 104.7 %copy-start.24 = (f32[192]{0:T(256)}, f32[192]{0:T(256)S(1)}, u32[]{:S(2)}) copy-start(f32[192]{0:T(256)S(1)} %fusion.130) | copy-start | bytes 2308
  5.8 62.1 %copy-start.16 = (f32[1,1,192,8,24]{2,4,0,3,1:T(8,128)}, f32[1,1,192,8,24]{2,4,0,3,1:T(8,128)S(1)}, u32[]{:S(2)}) copy-start(f32[1,1,192,8,24]{2,4,0,3,1:T(8,128)S(1)} %get-tuple-element.38) | copy-start | bytes 442372
  28.9 0.6 copy-start.12
  29.5 9.9 %copy-start.3 = (f32[96,24,192]{2,1,0:T(8,128)}, f32[96,24,192]{2,1,0:T(8,128)S(1)}, u32[]{:S(2)}) copy-start(f32[96,24,192]{2,1,0:T(8,128)S(1)} %maximum_divide_fusion) | copy-start | bytes 5308420
  29.5 9.9 %slice-start = ((s8[14155776]{0:T(1024)(128)(4,1)}), s8[4194304]{0:T(1024)(128)(4,1)S(1)}, s32[]{:S(2)}) async-start(s8[14155776]{0:T(1024)(128)(4,1)} %bitcast.253), calls=%async_computation.2 | async-start | bytes 8388608
  29.7 9.7 %copy-start.5 = (f32[96,24,192]{2,1,0:T(8,128)}, f32[96,24,192]{2,1,0:T(8,128)S(1)}, u32[]{:S(2)}) copy-start(f32[96,24,192]{2,1,0:T(8,128)S(1)} %and_convert_fusion) | copy-start | bytes 5308420
  29.7 10.8 %slice-start.1 = ((s8[14155776]{0:T(1024)(128)(4,1)}), s8[4194304]{0:T(1024)(128)(4,1)S(1)}, s32[]{:S(2)}) async-start(s8[14155776]{0:T(1024)(128)(4,1)} %bitcast.253), calls=%async_computation.3 | async-start | bytes 8388608
  29.7 13.6 %slice-start.2 = ((s8[14155776]{0:T(1024)(128)(4,1)}), s8[4194304]{0:T(1024)(128)(4,1)S(1)}, s32[]{:S(2)}) async-start(s8[14155776]{0:T(1024)(128)(4,1)} %bitcast.253), calls=%async_computation.4 | async-start | bytes 8388608
  29.7 14.0 %slice-start.3 = ((s8[14155776]{0:T(1024)(128)(4,1)}), s8[1572864]{0:T(1024)(128)(4,1)S(1)}, s32[]{:S(2)}) async-start(s8[14155776]{0:T(1024)(128)(4,1)} %bitcast.253), calls=%async_computation.5 | async-start | bytes 3145728
  39.4 21.6 %copy-start.1 = (f32[2,1,96,24,192]{4,3,2,1,0:T(8,128)}, f32[2,1,96,24,192]{4,3,2,1,0:T(8,128)S(1)}, u32[]{:S(2)}) copy-start(f32[2,1,96,24,192]{4,3,2,1,0:T(8,128)S(1)} %get-tuple-element.5) | copy-start | bytes 10616836
  49.8 11.2 %copy-start.2 = (f32[2,1,96,24,192]{4,3,2,0,1:T(8,128)}, f32[2,1,96,24,192]{4,3,2,0,1:T(8,128)S(1)}, u32[]{:S(2)}) copy-start(f32[2,1,96,24,192]{4,3,2,0,1:T(8,128)S(1)} %get-tuple-element.12) | copy-start | bytes 10616836
  56.0 5.0 slice-start.4
  58.7 2.3 slice-start.5
  95.7 161.4 %all-to-all-start = ((f32[8,2,24,24,360]{4,2,3,1,0:T(8,128)}), f32[8,2,24,24,360]{4,2,3,1,0:T(8,128)}, u32[]{:S(2)}, u32[]{:S(2)}) async-start(f32[8,2,24,24,360]{4,2,3,1,0:T(8,128)} %copy.83), calls=%async_computation | async-start | bytes 28311552 | tf_op jit(solution)/shard_map/all_to_all | solution.py:140
  108.1 168.3 %copy-start.20 = (f32[1,1,8,24,192]{4,3,0,2,1:T(8,128)}, f32[1,1,8,24,192]{4,3,0,2,1:T(8,128)S(1)}, u32[]{:S(2)}) copy-start(f32[1,1,8,24,192]{4,3,0,2,1:T(8,128)S(1)} %get-tuple-element.33) | copy-start | bytes 442372
  312.1 7.6 %copy-start.8 = (f32[1,24,1,72,192]{4,3,1,2,0:T(8,128)S(1)}, f32[1,24,1,72,192]{4,3,1,2,0:T(8,128)}, u32[]{:S(2)}) copy-start(f32[1,24,1,72,192]{4,3,1,2,0:T(8,128)} %get-tuple-element.19) | copy-start | bytes 3981316
  312.1 7.6 %copy-start.9 = (f32[1,24,1,72,192]{4,3,1,2,0:T(8,128)S(1)}, f32[1,24,1,72,192]{4,3,1,2,0:T(8,128)}, u32[]{:S(2)}) copy-start(f32[1,24,1,72,192]{4,3,1,2,0:T(8,128)} %get-tuple-element.20) | copy-start | bytes 3981316
  312.1 7.6 %copy-start.22 = (f32[1,96,192]{2,1,0:T(8,128)S(1)}, f32[1,96,192]{2,1,0:T(8,128)}, u32[]{:S(2)}) copy-start(f32[1,96,192]{2,1,0:T(8,128)} %get-tuple-element.48) | copy-start | bytes 221188
  312.1 7.6 %copy-start.23 = (f32[1,96,192]{2,1,0:T(8,128)S(1)}, f32[1,96,192]{2,1,0:T(8,128)}, u32[]{:S(2)}) copy-start(f32[1,96,192]{2,1,0:T(8,128)} %get-tuple-element.49) | copy-start | bytes 221188
  341.5 17.2 %copy-start.10 = (f32[192,1,96]{0,2,1:T(8,128)S(1)}, f32[192,1,96]{0,2,1:T(8,128)}, u32[]{:S(2)}) copy-start(f32[192,1,96]{0,2,1:T(8,128)} %get-tuple-element.50) | copy-start | bytes 221188
  341.5 17.2 %copy-start.11 = (f32[192,1,96]{0,2,1:T(8,128)S(1)}, f32[192,1,96]{0,2,1:T(8,128)}, u32[]{:S(2)}) copy-start(f32[192,1,96]{0,2,1:T(8,128)} %get-tuple-element.51) | copy-start | bytes 221188
  366.9 4.9 copy-start.14
  366.9 4.9 copy-start.15
  366.9 4.9 copy-start.17
  389.0 5.5 copy-start.13
  389.0 134.1 %all-to-all-start.1 = ((f32[8,2,24,24,216]{4,2,1,3,0:T(8,128)}), f32[8,2,24,24,216]{4,2,1,3,0:T(8,128)}, u32[]{:S(2)}, u32[]{:S(2)}) async-start(f32[8,2,24,24,216]{4,2,1,3,0:T(8,128)} %copy.100), calls=%async_computation.1 | async-start | bytes 18874368 | tf_op jit(solution)/shard_map/all_to_all | solution.py:186
  405.6 6.2 %copy-start.31 = (f32[96]{0:T(128)S(1)}, f32[96]{0:T(128)}, u32[]{:S(2)}) copy-start(f32[96]{0:T(128)} %copy-done.30) | copy-start | bytes 1156
  413.3 109.9 %copy-start.18 = (f32[1,1,8,24,192]{4,3,0,2,1:T(8,128)S(1)}, f32[1,1,8,24,192]{4,3,0,2,1:T(8,128)}, u32[]{:S(2)}) copy-start(f32[1,1,8,24,192]{4,3,0,2,1:T(8,128)} %get-tuple-element.29) | copy-start | bytes 442372
  413.3 109.9 %copy-start.19 = (f32[1,1,8,24,192]{4,3,0,2,1:T(8,128)S(1)}, f32[1,1,8,24,192]{4,3,0,2,1:T(8,128)}, u32[]{:S(2)}) copy-start(f32[1,1,8,24,192]{4,3,0,2,1:T(8,128)} %get-tuple-element.30) | copy-start | bytes 442372
  413.3 109.9 %copy-start.21 = (f32[1,1,8,24,192]{4,3,0,2,1:T(8,128)S(1)}, f32[1,1,8,24,192]{4,3,0,2,1:T(8,128)}, u32[]{:S(2)}) copy-start(f32[1,1,8,24,192]{4,3,0,2,1:T(8,128)} %copy-done.20) | copy-start | bytes 442372
  536.0 12.4 %copy-start.4 = (f32[96,24,192]{2,1,0:T(8,128)S(1)}, f32[96,24,192]{2,1,0:T(8,128)}, u32[]{:S(2)}) copy-start(f32[96,24,192]{2,1,0:T(8,128)} %copy-done.3) | copy-start | bytes 5308420
  536.0 12.4 %copy-start.25 = (f32[192]{0:T(256)S(1)}, f32[192]{0:T(256)}, u32[]{:S(2)}) copy-start(f32[192]{0:T(256)} %copy-done.24) | copy-start | bytes 2308
  536.0 12.4 %copy-start.27 = (f32[24]{0:T(128)S(1)}, f32[24]{0:T(128)}, u32[]{:S(2)}) copy-start(f32[24]{0:T(128)} %copy-done.26) | copy-start | bytes 292
  536.0 12.4 %copy-start.29 = (f32[96]{0:T(128)S(1)}, f32[96]{0:T(128)}, u32[]{:S(2)}) copy-start(f32[96]{0:T(128)} %copy-done.28) | copy-start | bytes 1156
  548.5 10.6 %copy-start = (f32[2,216,24,192]{3,2,1,0:T(8,128)S(1)}, f32[2,216,24,192]{3,2,1,0:T(8,128)}, u32[]{:S(2)}) copy-start(f32[2,216,24,192]{3,2,1,0:T(8,128)} %copy.102) | copy-start | bytes 23887876
  548.5 11.3 %copy-start.6 = (f32[96,24,192]{2,1,0:T(8,128)S(1)}, f32[96,24,192]{2,1,0:T(8,128)}, u32[]{:S(2)}) copy-start(f32[96,24,192]{2,1,0:T(8,128)} %copy-done.5) | copy-start | bytes 5308420
  575.4 5.7 copy-start.7
where the time goes:
time: 607 us; the launch traced here: 596 us
  waiting for transfers between devices  149 us (25%)
  local copies, waits for them, and re-layouts  132 us (22%)
  other arithmetic  102 us (17%)
  blocking collectives  98 us (16%)
  matrix products  96.7 us (16%)
  starting transfers between devices  11.2 us (2%)
  between operations  6.98 us (1%)
    all_to_all x1, waiting for transfers between devices, on_device(): lax.all_to_all(slab_spread(fields, group_size, slab_width, inverse_table)...  149 us
    psum x1, blocking collectives, on_device(): summed = lax.psum(local_squares, ('py', 'pz'))  83.7 us
    another operation x6, local copies, waits for them, and re-layouts, project(): jnp.stack([keep_mask * (field[:, axis_index] - waves[axis_index] * normal...  33.3 us
    mul x4, other arithmetic, project(): keep_mask * (field[:, axis_index] - waves[axis_index] * normal_part * inv...  29.3 us
    dot_general x2, matrix products, slab_rows(): jnp.einsum('grxlm,rsgly->sxmy', received, table.reshape(2, 2, group_size,...  26.7 us
    dot_general x1, matrix products, on_device(): jnp.einsum('sxcjy,sjz->cxyz', strips, backward_cut, precision=highest)  21.9 us
    reduce_max x1, other arithmetic, on_device(): jnp.max(jnp.abs(velocity[0]) + jnp.abs(velocity[1]) + jnp.abs(velocity[2]))  17.2 us
    transpose x1, local copies, waits for them, and re-layouts, slab_rows(): jnp.einsum('grxlm,rsgly->sxmy', received, table.reshape(2, 2, group_size,...  16.9 us
  transfers between devices with their start and end apart: 2, of which 1 were waited for; matrix products, arithmetic and copies ran while one was open for 6% of the time, Pallas kernels for 0%

commit v1 on v0

v1 whole, which is shorter than its diff:
```python
import functools
import math

import jax
import jax.numpy as jnp
import numpy as np
from jax import lax
from jax.experimental import pallas as pl
from jax.experimental.pallas import tpu as pltpu
from jax.sharding import PartitionSpec as P

viscosity = 0.004
high = lax.Precision.HIGH
TILE = 8
LANES = 128
GROUP = ("py", "pz")
f32 = jnp.float32
bf16 = jnp.bfloat16


def halves(table):
    table = np.asarray(table, np.float32)
    top = table.astype(jnp.bfloat16)
    rest = (table - top.astype(np.float32)).astype(jnp.bfloat16)
    return top, rest


def split(value):
    top = value.astype(bf16)
    return top, (value - top.astype(f32)).astype(bf16)


def signed(index, points):
    return np.where(index < points // 2, index, index - points)


class Sizes:
    def __init__(self, points, group, cross):
        self.points = points
        self.group = group
        self.cross = cross
        self.limit = points // 3
        self.slab = points // group
        self.planes = TILE if self.slab % TILE == 0 else self.slab
        self.chunks = self.slab // self.planes
        self.rows = cross * TILE
        self.window = -(-points // LANES) * LANES
        self.start = (points // LANES) * LANES
        self.pair = 2 * points
        self.above = -(-(self.limit + 1) // cross)
        self.below = -(-self.limit // cross)
        self.scale = float(points) ** -1.5
        assert self.planes <= TILE and 2 * self.limit == LANES and cross % 2 == 0
        assert self.pair % LANES == 0 and self.start + self.window == self.pair

    def pairs_of(self, device):
        mirrored = device >= self.group // 2
        block = self.group - 1 - device if mirrored else device
        kept = self.limit + (0 if mirrored else 1) - block * self.cross
        return -(-min(max(kept, 0), self.cross) // 2)

    def planes_of(self, chunk):
        place = np.arange(TILE)
        plane = np.arange(self.group)[:, None] * self.slab + chunk * self.planes + place
        return np.where(place < self.planes, plane, -1)

    def windows(self, planes):
        lane = np.arange(self.window)
        both = []
        for which, begin in enumerate((0, self.start)):
            index = begin + lane - which * self.points
            wave = signed(index, self.points)
            live = (index >= 0) & (index < self.points) & (np.abs(wave) <= self.limit)
            live = live[None, :] & (planes >= 0)[:, None]
            angle = 2.0 * np.pi * ((planes[:, None] * wave[None, :]) % self.points) / self.points
            both.append((live * np.cos(angle), live * np.sin(angle), live * wave[None, :]))
        return both

    def spread_table(self, chunk):
        tables = []
        for cosine, sine, wave in self.windows(self.planes_of(chunk).reshape(-1)):
            tables.append(np.concatenate([cosine, sine, -wave * sine, wave * cosine]))
        return halves(np.stack(tables))

    def close_table(self):
        planes = np.stack([self.planes_of(c) for c in range(self.chunks)], axis=1).reshape(-1)
        return halves(np.stack([np.concatenate([c, s], axis=1) for c, s, _ in self.windows(planes)]))

    def angle(self, rows, cols):
        return 2.0 * np.pi * (np.outer(rows, cols) % self.points) / self.points

    def cross_tables(self):
        wave = np.arange(1, self.limit + 1)
        angle = self.angle(np.arange(self.points), wave)
        top, rest = halves(np.concatenate([np.cos(angle), np.sin(angle)], axis=1))
        back_top, back_rest = halves(np.concatenate([np.cos(angle), np.sin(angle)], axis=1).T)
        return (np.concatenate([top, top], axis=1), rest, back_top, back_rest)

    def depth_tables(self):
        wave = np.arange(1, self.limit + 1)
        angle = self.angle(wave, np.arange(self.points))
        waves = np.concatenate([np.cos(angle), -np.sin(angle)])
        top, rest = halves(2.0 * self.scale * waves)
        ones = np.ones((LANES, self.points), jnp.bfloat16)
        back_top, back_rest = halves(self.scale * waves.T)
        return (
            np.concatenate([top, top]),
            np.concatenate([rest, ones]),
            np.concatenate([back_top, back_rest], axis=1),
            back_top,
        )


def dot(left, right):
    return jnp.dot(left, right, preferred_element_type=f32)


def dot_rows(left, right):
    return lax.dot_general(left, right, (((1,), (1,)), ((), ())), preferred_element_type=f32)


def turn(value):
    lane = lax.broadcasted_iota(jnp.int32, (1, LANES), 1)
    sign = jnp.where(lane < LANES // 2, -1.0, 1.0).astype(f32)
    return pltpu.roll(value, LANES // 2, 1) * sign


def pair_waves(size, first_cross, cutoffs):
    lane = lax.broadcasted_iota(jnp.int32, (1, size.pair), 1)
    second = (lane >= size.points).astype(jnp.int32)
    along = lane - second * size.points
    along = jnp.where(along < size.points // 2, along, along - size.points)
    cross = first_cross + second
    cross = jnp.where(cross < size.points // 2, cross, cross - size.points)
    depth = lax.broadcasted_iota(jnp.int32, (size.limit, 1), 0) + 1
    keep = (jnp.abs(along) <= cutoffs[0]) & (jnp.abs(cross) <= cutoffs[1])
    keep = keep.astype(f32) * (depth <= cutoffs[2]).astype(f32)
    waves = (along.astype(f32), cross.astype(f32), depth.astype(f32))
    square = waves[0] * waves[0] + waves[1] * waves[1] + waves[2] * waves[2]
    return waves, square, keep


def projected(waves, square, keep, field):
    normal = waves[0] * field[0] + waves[1] * field[1] + waves[2] * field[2]
    normal = normal * (1.0 / jnp.maximum(square, 1.0))
    return [keep * (field[i] - waves[i] * normal) for i in range(3)]


def spread_pair(size, first_cross, mirrored, cutoffs, fields, top_ref, rest_ref, o_ref, base_row):
    waves, square, keep = pair_waves(size, first_cross, cutoffs)
    parts = [projected(waves, square, keep, fields[r]) for r in range(2)]
    whole = [jnp.concatenate([parts[0][i], parts[1][i]], axis=0) for i in range(3)]
    tops, rests = zip(*[split(w) for w in whole])
    count = size.group * TILE
    for which, begin in enumerate((0, size.start)):
        lanes = slice(begin, begin + size.window)
        top, rest = top_ref[which], rest_ref[which]
        x_top, x_rest = tops[0][:, lanes], rests[0][:, lanes]
        ahead = dot_rows(top[: 2 * count], x_top) + dot_rows(top[: 2 * count], x_rest)
        ahead = ahead + dot_rows(rest[: 2 * count], x_top)
        o_top = jnp.concatenate([tops[1][:, lanes], tops[2][:, lanes]], axis=0)
        o_rest = jnp.concatenate([rests[1][:, lanes], rests[2][:, lanes]], axis=0)
        other = dot_rows(top, o_top) + dot_rows(top, o_rest) + dot_rows(rest, o_top)
        results = [ahead[:count] + turn(ahead[count:])]
        for base in (0, 2 * count):
            for i in range(2):
                cols = slice(i * LANES, (i + 1) * LANES)
                results.append(
                    other[base : base + count, cols]
                    + turn(other[base + count : base + 2 * count, cols])
                )
        slot = which + mirrored - 2 * which * mirrored
        at = pl.ds(pl.multiple_of(base_row + slot * TILE, TILE), TILE)
        for g in range(size.group):
            for i in range(5):
                o_ref[g, i, at, :] = results[i][g * TILE : (g + 1) * TILE]


def layer_ahead(size, e_ref, first_row, cross_refs, above, below):
    cross, limit, group = size.cross, size.limit, size.group
    for m in range(size.above):
        above[0, m * cross : (m + 1) * cross, :] = e_ref[m, pl.ds(first_row, cross), :]
    for m in range(size.below):
        below[0, m * cross : (m + 1) * cross, :] = e_ref[group - 1 - m, pl.ds(first_row, cross), :]
    plus, minus = above[0, 1 : limit + 1, :], below[0, :limit, :]
    data = jnp.concatenate([plus + minus, turn(plus - minus)], axis=0)
    top, rest = split(data)
    real = dot(cross_refs[0][...], jnp.concatenate([top, rest], axis=0)) + dot(cross_refs[1][...], top)
    real = (real + above[0, 0:1, :]) * size.scale
    top = real.astype(bf16).astype(f32)
    lane = lax.broadcasted_iota(jnp.int32, (1, LANES), 1)
    return jnp.where(lane < LANES // 2, top, pltpu.roll(real - top, LANES // 2, 1)).astype(bf16)


def layer_back(size, sums, cross_refs):
    limit = size.limit
    top, rest = split(sums)
    waves = dot(cross_refs[2][...], top) + dot(cross_refs[2][...], rest) + dot(cross_refs[3][...], top)
    even, odd = waves[:limit], pltpu.roll(waves[limit:], LANES // 2, 1)
    return even - odd, even + odd, jnp.sum(sums, axis=0, keepdims=True)


def middle_plane(size, plane, r_ref, extra, cross_refs, depth_refs, o_ref, x_ref, s_ref, scratch):
    ya_ref, yb_ref, yc_ref, yd_ref = cross_refs
    za_ref, zb_ref, zc_ref, zd_ref = depth_refs
    above, below, back_above, back_below = scratch
    limit, cross, group, points = size.limit, size.cross, size.group, size.points
    at = pl.ds(plane, cross, stride=TILE)
    sums, turned, firsts = [], [], []
    for i in range(5):
        for m in range(size.above):
            above[i, m * cross : (m + 1) * cross, :] = r_ref[m, i, at, :]
        for m in range(size.below):
            below[i, m * cross : (m + 1) * cross, :] = r_ref[group - 1 - m, i, at, :]
        plus = above[i, 1 : limit + 1, :]
        minus = below[i, :limit, :]
        sums.append(plus + minus)
        turned.append(turn(plus - minus))
        firsts.append(jnp.broadcast_to(above[i, 0:1, :], (TILE, LANES)))
    k = (lax.broadcasted_iota(jnp.int32, (limit, 1), 0) + 1).astype(f32)
    lane = lax.broadcasted_iota(jnp.int32, (1, LANES), 1)
    deep = (lane % limit + 1).astype(f32)
    all_sums = sums[:3] + [
        k * turned[2] - deep * turn(sums[1]),
        deep * turn(sums[0]) - sums[4],
        sums[3] - k * turned[0],
    ]
    all_turned = turned[:3] + [
        -k * sums[2] - deep * turn(turned[1]),
        deep * turn(turned[0]) - turned[4],
        turned[3] + k * sums[0],
    ]
    firsts = firsts[:3] + [
        -deep * turn(firsts[1]),
        deep * turn(firsts[0]) - firsts[4],
        firsts[3],
    ]
    data = jnp.concatenate(
        [jnp.concatenate([all_sums[i], all_turned[i]], axis=0) for i in range(6)], axis=1
    )
    first = jnp.concatenate([f[0:1] for f in firsts], axis=1)
    top, rest = split(data)
    strips = dot(ya_ref[...], jnp.concatenate([top, rest], axis=0)) + dot(yb_ref[...], top) + first
    physical = []
    for i in range(6):
        top, rest = split(strips[:, i * LANES : (i + 1) * LANES])
        mine = ((lane % (LANES // 2)) == i * TILE + plane).astype(f32).astype(bf16)
        physical.append(
            dot(jnp.concatenate([top, rest], axis=1), za_ref[...])
            + dot(jnp.concatenate([top, extra * mine], axis=1), zb_ref[...])
        )
    v, w = physical[:3], physical[3:]
    speed = jnp.abs(v[0]) + jnp.abs(v[1]) + jnp.abs(v[2])
    power = v[0] * v[0] + v[1] * v[1] + v[2] * v[2]
    s_ref[0] = jnp.maximum(s_ref[0], jnp.max(speed.reshape(-1, TILE, points), axis=0))
    s_ref[1] = s_ref[1] + jnp.sum(power.reshape(-1, TILE, points), axis=0)
    nonlinear = [
        v[1] * w[2] - v[2] * w[1],
        v[2] * w[0] - v[0] * w[2],
        v[0] * w[1] - v[1] * w[0],
    ]
    deeps = []
    kept = x_ref[...]
    for i in range(3):
        top, rest = split(nonlinear[i])
        both = dot(top, zc_ref[...])
        deeps.append(both[:, :LANES] + both[:, LANES:] + dot(rest, zd_ref[...]))
        total = jnp.sum(nonlinear[i], axis=1, keepdims=True) * size.scale
        kept = jnp.where(lane == i * TILE + plane, total, kept)
    x_ref[...] = kept
    data = jnp.concatenate(deeps, axis=1)
    top, rest = split(data)
    waves = dot(yc_ref[...], top) + dot(yc_ref[...], rest) + dot(yd_ref[...], top)
    first = jnp.sum(data, axis=0, keepdims=True)
    for i in range(3):
        lanes = slice(i * LANES, (i + 1) * LANES)
        even, odd = waves[:limit, lanes], turn(waves[limit:, lanes])
        back_above[i, 0:1, :] = first[:, lanes]
        back_above[i, 1 : limit + 1, :] = even - odd
        back_below[i, :limit, :] = even + odd
        for m in range(size.above):
            o_ref[m, i, at, :] = back_above[i, m * cross : (m + 1) * cross, :]
        for m in range(size.below):
            o_ref[group - 1 - m, i, at, :] = back_below[i, m * cross : (m + 1) * cross, :]


def section_kernel(size, minor, cut_ref, e_ref, v_ref, top_ref, rest_ref, ya, yb, yc, yd, za, zb, zc, zd,
                   out_ref, last_ref, v_buf, send, recv, e_recv, back, last, sums, stats,
                   above, below, back_above, back_below, v_sem, e_sems, go_sems, come_sems,
                   back_go, back_come, last_go, last_come, own_sems):
    group, cross, chunks, limit = size.group, size.cross, size.chunks, size.limit
    steps = cross // 2
    me = lax.axis_index("py") * minor + lax.axis_index("pz")
    half = group // 2
    mirrored = (me >= half).astype(jnp.int32)
    counts = [size.pairs_of(g) for g in range(group)]
    classes = sorted(set(counts))

    def pairs_at(device):
        block = jnp.where(device >= half, group - 1 - device, device)
        kept = limit + jnp.where(device >= half, 0, 1) - block * cross
        return (jnp.clip(kept, 0, cross) + 1) // 2

    mine = pairs_at(me)
    cutoffs = (cut_ref[0], cut_ref[1], cut_ref[2])
    cross_refs, depth_refs = (ya, yb, yc, yd), (za, zb, zc, zd)
    scratch = (above, below, back_above, back_below)

    def peer(device):
        return {"py": device // minor, "pz": device % minor}

    def peers():
        return [(off, (me + off) % group) for off in range(1, group)]

    def remote(src, dst, go, come, device):
        return pltpu.make_async_remote_copy(
            src_ref=src, dst_ref=dst, send_sem=go, recv_sem=come,
            device_id=peer(device), device_id_type=pl.DeviceIdType.MESH,
        )

    def fetch(p, slot):
        j = p + mirrored * (steps - 1 - 2 * p)
        lanes = pl.ds(pl.multiple_of(j * size.pair, LANES), size.pair)
        return pltpu.make_async_copy(
            v_ref.at[:, :, 0 : v_buf.shape[3], lanes], v_buf.at[slot], v_sem.at[slot]
        )

    @pl.when(mine > 0)
    def _():
        fetch(0, 0).start()

    barrier = pltpu.get_barrier_semaphore()
    for _, device in peers():
        pl.semaphore_signal(barrier, inc=1, device_id=peer(device), device_id_type=pl.DeviceIdType.MESH)
    pl.semaphore_wait(barrier, group - 1)

    def layer_copy(off, device):
        return remote(e_ref.at[device], e_recv.at[me], e_sems.at[0, off], e_sems.at[1, me], device)

    for off, device in peers():
        layer_copy(off, device).start()
    own_layer = pltpu.make_async_copy(e_ref.at[me], e_recv.at[me], own_sems.at[0])
    own_layer.start()

    back_above[...] = jnp.zeros_like(back_above)
    back_below[...] = jnp.zeros_like(back_below)
    back[...] = jnp.zeros_like(back)
    sums[...] = jnp.zeros_like(sums)
    stats[...] = jnp.zeros_like(stats)
    last[...] = jnp.zeros_like(last)

    def spread_step(t, carry):
        chunk, p = t // steps, t % steps

        @pl.when(p < mine)
        def _():
            slot = (chunk * mine + p) % 2
            fetch(p, slot).wait()
            following = jnp.where(p + 1 < mine, p + 1, 0)

            @pl.when((p + 1 < mine) | (chunk + 1 < chunks))
            def _():
                fetch(following, 1 - slot).start()

            j = p + mirrored * (steps - 1 - 2 * p)
            fields = [[v_buf[slot, r, i, 1 : limit + 1, :] for i in range(3)] for r in range(2)]
            spread_pair(
                size, me * cross + 2 * j, mirrored, cutoffs, fields,
                top_ref.at[chunk], rest_ref.at[chunk], send.at[chunk], p * 2 * TILE,
            )
            rows = pl.ds(pl.multiple_of(p * 2 * TILE, 2 * TILE), 2 * TILE)
            for off, device in peers():
                remote(
                    send.at[chunk, device, :, rows, :], recv.at[chunk, me, :, rows, :],
                    go_sems.at[chunk, off], come_sems.at[chunk, me], device,
                ).start()
            pltpu.make_async_copy(
                send.at[chunk, me, :, rows, :], recv.at[chunk, me, :, rows, :], come_sems.at[chunk, me]
            ).start()

        return carry

    lax.fori_loop(0, chunks * steps, spread_step, 0)

    def come_wait(chunk, g):
        ref = recv.at[chunk, g, :, 0 : counts[g] * 2 * TILE, :]
        pltpu.make_async_copy(ref, ref, come_sems.at[chunk, g]).wait()

    def middle_chunk(chunk, carry):
        for g in range(group):
            if counts[g]:
                come_wait(chunk, g)

        @pl.when(chunk == 0)
        def _():
            own_layer.wait()
            for off in range(1, group):
                source = (me + off) % group
                ref = e_recv.at[source]
                pltpu.make_async_copy(ref, ref, e_sems.at[1, source]).wait()

        extra = layer_ahead(size, e_recv, chunk * cross, cross_refs, above, below)

        def plane_step(plane, carry):
            middle_plane(
                size, plane, recv.at[chunk], extra, cross_refs, depth_refs,
                back.at[chunk], sums.at[chunk], stats, scratch,
            )
            return carry

        lax.fori_loop(0, size.planes, plane_step, 0)
        for off, device in peers():
            for n in classes:
                if n:
                    @pl.when(pairs_at(device) == n)
                    def _(n=n, off=off, device=device):
                        rows = slice(0, n * 2 * TILE)
                        remote(
                            back.at[chunk, device, :, rows, :], out_ref.at[chunk, me, :, rows, :],
                            back_go.at[chunk, off], back_come.at[chunk, me], device,
                        ).start()

        for n in classes:
            if n:
                @pl.when(mine == n)
                def _(n=n):
                    rows = slice(0, n * 2 * TILE)
                    pltpu.make_async_copy(
                        back.at[chunk, me, :, rows, :], out_ref.at[chunk, me, :, rows, :],
                        back_come.at[chunk, me],
                    ).start()

        plus, minus, first = layer_back(size, sums[chunk], cross_refs)
        back_above[0, 1 : limit + 1, :] = plus
        back_above[0, 0:1, :] = first
        back_below[0, :limit, :] = minus
        here = pl.ds(chunk * cross, cross)
        for m in range(size.above):
            last[m, here, :] = back_above[0, m * cross : (m + 1) * cross, :]
        for m in range(size.below):
            last[group - 1 - m, here, :] = back_below[0, m * cross : (m + 1) * cross, :]
        return carry

    lax.fori_loop(0, chunks, middle_chunk, 0)
    fastest = jnp.max(stats[0], axis=(0, 1), keepdims=True)
    squares = jnp.sum(stats[1], axis=(0, 1), keepdims=True)
    lane = lax.broadcasted_iota(jnp.int32, (TILE, LANES), 1)
    both = jnp.where(lane == 0, fastest, squares)
    for g in range(group):
        last[g, chunks * cross :, :] = both

    def last_copy(off, device):
        return remote(last.at[device], last_ref.at[me], last_go.at[off], last_come.at[me], device)

    for off, device in peers():
        last_copy(off, device).start()
    own_last = pltpu.make_async_copy(last.at[me], last_ref.at[me], own_sems.at[1])
    own_last.start()

    for off, device in peers():
        layer_copy(off, device).wait_send()
        last_copy(off, device).wait_send()
        ref = last_ref.at[device]
        pltpu.make_async_copy(ref, ref, last_come.at[device]).wait()
    own_last.wait()
    for n in classes:
        if n:
            rows = slice(0, n * 2 * TILE)

            @pl.when(mine == n)
            def _(n=n, rows=rows):
                def sent(chunk, carry):
                    for off in range(1, group):
                        ref = send.at[chunk, off, :, rows, :]
                        pltpu.make_async_copy(ref, ref, go_sems.at[chunk, off]).wait()
                    for g in range(group):
                        ref = out_ref.at[chunk, g, :, rows, :]
                        pltpu.make_async_copy(ref, ref, back_come.at[chunk, g]).wait()
                    return carry

                lax.fori_loop(0, chunks, sent, 0)

    def back_sent(chunk, carry):
        for off, device in peers():
            for n in classes:
                if n:
                    @pl.when(pairs_at(device) == n)
                    def _(n=n, off=off, device=device):
                        ref = back.at[chunk, device, :, 0 : n * 2 * TILE, :]
                        pltpu.make_async_copy(ref, ref, back_go.at[chunk, off]).wait()
        return carry

    lax.fori_loop(0, chunks, back_sent, 0)


def close_kernel(size, place_ref, scalar_ref, v_ref, first_ref, top_ref, rest_ref, *refs):
    r_ref, o_ref = refs
    step = pl.program_id(0)
    limit = size.limit
    results = [[[], []], [[], []], [[], []]]
    for which in range(2):
        slot = jnp.where(place_ref[1] == 1, 1 - which, which)
        at = pl.ds(pl.multiple_of(slot * TILE, TILE), TILE)
        for i in range(3):
            rows = jnp.concatenate(
                [r_ref[c, g, i, at, :] for g in range(size.group) for c in range(size.chunks)], axis=0
            )
            top, rest = split(rows.T)
            out = dot(top, top_ref[which]) + dot(top, rest_ref[which]) + dot(rest, top_ref[which])
            cosine, sine = out[:, : size.window], out[:, size.window :]
            results[i][0].append(cosine[:limit] + sine[limit:])
            results[i][1].append(cosine[limit:] - sine[:limit])

    def joined(low, high_part):
        begin = size.start
        if begin == size.window:
            return jnp.concatenate([low, high_part], axis=1)
        shared = size.window - begin
        return jnp.concatenate(
            [low[:, :begin], low[:, begin:] + high_part[:, :shared], high_part[:, shared:]], axis=1
        )

    waves, square, keep = pair_waves(
        size, place_ref[0] + 2 * step, (place_ref[2], place_ref[3], place_ref[4])
    )
    forcing, step_size = scalar_ref[0], scalar_ref[1]
    gain = 1.0 + step_size * (forcing - viscosity * square)
    depth = o_ref.shape[2]
    for r in range(2):
        solenoidal = projected(
            waves, square, keep, [v_ref[r, i, 1 : limit + 1, :] for i in range(3)]
        )
        forced = projected(waves, square, keep, [joined(*results[i][r]) for i in range(3)])
        for i in range(3):
            o_ref[r, i, 0:1, :] = first_ref[r * 3 + i : r * 3 + i + 1, :]
            o_ref[r, i, 1 : limit + 1, :] = solenoidal[i] * gain + jnp.where(keep > 0.0, step_size * forced[i], 0.0)
            o_ref[r, i, limit + 1 :, :] = jnp.zeros((depth - limit - 1, size.pair), f32)


def whole_block(array):
    return pl.BlockSpec(array.shape, lambda *_: (0,) * array.ndim)


def cost(flops, moved):
    return pl.CostEstimate(flops=int(flops), bytes_accessed=int(moved), transcendentals=0)


def params(megabytes=58):
    return pltpu.CompilerParams(
        dimension_semantics=("arbitrary",), vmem_limit_bytes=megabytes * 1024 * 1024
    )


def section(size, minor, cutoffs, layer, velocity):
    group, chunks, cross, points = size.group, size.chunks, size.cross, size.points
    tops, rests = zip(*[size.spread_table(c) for c in range(chunks)])
    tables = [np.stack(tops), np.stack(rests), *size.cross_tables(), *size.depth_tables()]
    ins = [cutoffs, layer, velocity, *[jnp.asarray(t) for t in tables]]
    kept_rows = -(-(size.limit + 1) // TILE) * TILE
    above = -(-max(size.above * cross, size.limit + 1) // TILE) * TILE
    below = -(-max(size.below * cross, size.limit) // TILE) * TILE
    last_rows = chunks * cross + TILE
    vmem = pl.BlockSpec(memory_space=pltpu.VMEM)
    anywhere = pl.BlockSpec(memory_space=pl.ANY)
    dma = pltpu.SemaphoreType.DMA
    return pl.pallas_call(
        functools.partial(section_kernel, size, minor),
        in_specs=[pl.BlockSpec(memory_space=pltpu.SMEM), vmem, anywhere] + [vmem] * len(tables),
        out_specs=[anywhere, anywhere],
        out_shape=[
            jax.ShapeDtypeStruct((chunks, group, 3, size.rows, LANES), f32),
            jax.ShapeDtypeStruct((group, last_rows, LANES), f32),
        ],
        scratch_shapes=[
            pltpu.VMEM((2, 2, 3, kept_rows, size.pair), f32),
            pltpu.VMEM((chunks, group, 5, size.rows, LANES), f32),
            pltpu.VMEM((chunks, group, 5, size.rows, LANES), f32),
            pltpu.VMEM((group, chunks * cross, LANES), f32),
            pltpu.VMEM((chunks, group, 3, size.rows, LANES), f32),
            pltpu.VMEM((group, last_rows, LANES), f32),
            pltpu.VMEM((chunks, points, LANES), f32),
            pltpu.VMEM((2, TILE, points), f32),
            pltpu.VMEM((5, above, LANES), f32),
            pltpu.VMEM((5, below, LANES), f32),
            pltpu.VMEM((3, above, LANES), f32),
            pltpu.VMEM((3, below, LANES), f32),
            dma((2,)),
            dma((2, group)),
            dma((chunks, group)),
            dma((chunks, group)),
            dma((chunks, group)),
            dma((chunks, group)),
            dma((group,)),
            dma((group,)),
            dma((2,)),
        ],
        compiler_params=pltpu.CompilerParams(
            collective_id=0, has_side_effects=True, vmem_limit_bytes=60 * 1024 * 1024
        ),
        cost_estimate=cost(5e10, 4e7),
        name="section",
    )(*ins)


def close(size, place, scalars, velocity, first, returned):
    top, rest = (jnp.asarray(t) for t in size.close_table())
    steps = size.cross // 2
    block = (2, 3, velocity.shape[2], size.pair)
    return pl.pallas_call(
        functools.partial(close_kernel, size),
        grid_spec=pltpu.PrefetchScalarGridSpec(
            num_scalar_prefetch=1,
            grid=(steps,),
            in_specs=[
                pl.BlockSpec(memory_space=pltpu.SMEM),
                pl.BlockSpec((2, 3, -(-(size.limit + 1) // TILE) * TILE, size.pair), lambda j, p: (0, 0, 0, j)),
                pl.BlockSpec((6, size.pair), lambda j, p: (0, j)),
                whole_block(top),
                whole_block(rest),
                pl.BlockSpec(
                    (size.chunks, size.group, 3, 2 * TILE, LANES),
                    lambda j, p: (0, 0, 0, jnp.where(p[1] == 1, steps - 1 - j, j), 0),
                ),
            ],
            out_specs=pl.BlockSpec(block, lambda j, p: (0, 0, 0, j)),
        ),
        out_shape=jax.ShapeDtypeStruct(velocity.shape, f32),
        compiler_params=params(),
        cost_estimate=cost(5e9, 4e7),
        name="close",
    )(place, scalars, velocity, first, top, rest, returned)


class Shallow:
    def __init__(self, size, velocity, cutoffs, device):
        self.size = size
        points, cross = size.points, size.cross
        layer = velocity[:, :, 0, :].reshape(2, 3, cross, points)
        along = jnp.asarray(signed(np.arange(points), points), jnp.int32)[None, :]
        mirrored = device >= size.group // 2
        spot = lax.broadcasted_iota(jnp.int32, (cross, 1), 0)
        layer = jnp.where(mirrored, layer[:, :, ::-1], layer)
        index = device * cross + jnp.where(mirrored, cross - 1 - spot, spot)
        self.mirrored = mirrored
        across = jnp.where(index < points // 2, index, index - points)
        keep = (jnp.abs(along) <= cutoffs[0]) & (jnp.abs(across) <= cutoffs[1]) & (cutoffs[2] >= 0)
        self.keep = keep.astype(f32)
        self.waves = (along.astype(f32), across.astype(f32), jnp.zeros((1, 1), f32))
        self.square = self.waves[0] ** 2 + self.waves[1] ** 2
        self.layer = jnp.stack(
            [jnp.stack(projected(self.waves, self.square, self.keep, layer[r])) for r in range(2)]
        )
        planes = np.stack([size.planes_of(c) for c in range(size.chunks)], axis=1)
        self.live = (planes >= 0).reshape(-1)
        angle = size.angle(signed(np.arange(points), points), planes.reshape(-1))
        self.cosine = (np.cos(angle) * self.live).astype(np.float32)
        self.sine = (np.sin(angle) * self.live).astype(np.float32)

    def ahead(self):
        size = self.size
        group, chunks, cross = size.group, size.chunks, size.cross

        def turned(x):
            return jnp.stack([-x[1], x[0]])

        u = self.layer
        along, across = self.waves[0], self.waves[1]
        six = jnp.stack(
            [u[:, 0], u[:, 1], u[:, 2], turned(across * u[:, 2]), -turned(along * u[:, 2]),
             turned(along * u[:, 1] - across * u[:, 0])],
            axis=1,
        )
        table = np.concatenate([self.cosine, self.sine], axis=1)
        out = jnp.einsum("rflk,kp->rflp", six, table, precision=high)
        half = self.cosine.shape[1]
        cosine, sine = out[..., :half], out[..., half:]
        grid = jnp.stack([cosine[0] - sine[1], cosine[1] + sine[0]])
        grid = jnp.transpose(grid.reshape(2, 6, cross, group, chunks, TILE), (3, 4, 2, 0, 1, 5))
        grid = grid.reshape(group, chunks * cross, 2, 6 * TILE)
        grid = jnp.pad(grid, ((0, 0), (0, 0), (0, 0), (0, LANES // 2 - 6 * TILE)))
        return grid.reshape(group, chunks * cross, LANES)

    def back(self, got):
        size = self.size
        group, chunks, cross, points = size.group, size.chunks, size.cross, size.points
        numbers = got[:, chunks * cross, :2]
        fastest, squares = jnp.max(numbers[:, 0]), jnp.sum(numbers[:, 1])
        rows = got[:, : chunks * cross].reshape(group, chunks, cross, 2, LANES // 2)
        rows = rows[..., : 3 * TILE].reshape(group, chunks, cross, 2, 3, TILE)
        rows = jnp.transpose(rows, (3, 4, 2, 0, 1, 5)).reshape(2, 3, cross, group * chunks * TILE)
        table = np.concatenate([self.cosine.T, self.sine.T], axis=1)
        out = jnp.einsum("rflp,pk->rflk", rows, table, precision=high)
        cosine, sine = out[..., :points], out[..., points:]
        forced = jnp.stack([cosine[0] + sine[1], cosine[1] - sine[0]])
        forced = jnp.stack(
            [jnp.stack(projected(self.waves, self.square, self.keep, forced[r])) for r in range(2)]
        )
        return forced, fastest, squares


def on_device(velocity, time_step, power, cutoffs):
    group = lax.axis_size("py") * lax.axis_size("pz")
    points = 2 * velocity.shape[2]
    size = Sizes(points, group, velocity.shape[3] // points)
    device = lax.axis_index(GROUP)
    place = jnp.stack(
        [device * size.cross, (device >= group // 2).astype(jnp.int32), cutoffs[0], cutoffs[1], cutoffs[2]]
    ).astype(jnp.int32)
    shallow = Shallow(size, velocity, cutoffs, device)
    returned, got = section(size, lax.axis_size("pz"), cutoffs, shallow.ahead(), velocity)
    forced, fastest, squares = shallow.back(got)
    step_size = time_step[0]
    energy = 0.5 * squares / float(points**3)
    forcing = power[0] / jnp.maximum(2.0 * energy, 0.5)
    gain = 1.0 + step_size * (forcing - viscosity * shallow.square)
    first = shallow.layer * gain + jnp.where(shallow.keep > 0.0, step_size * forced, 0.0)
    first = jnp.where(shallow.mirrored, first[:, :, ::-1], first).reshape(6, size.cross * points)
    velocity_next = close(
        size, place, jnp.stack([forcing, step_size]), velocity, first, returned
    )
    cfl = step_size * fastest * points / (2.0 * math.pi)
    return velocity_next, cfl.reshape(1), energy.reshape(1)


def solution(mesh):
    return jax.shard_map(
        on_device,
        mesh=mesh,
        in_specs=(P("member", None, None, ("py", "pz")), P("member"), P("member"), P("member")),
        out_specs=(P("member", None, None, ("py", "pz")), P("member"), P("member")),
        check_vma=False,
    )
```

time: 607 us -> 222 us (0.37); the launches traced: 596 us -> 219 us
  Pallas kernels: 0 us -> 196 us
  waiting for transfers between devices: 149 us -> 0 us
  local copies, waits for them, and re-layouts: 132 us -> 8.62 us
  blocking collectives: 98 us -> 0 us
  other arithmetic: 102 us -> 6.32 us
  matrix products: 96.7 us -> 1.04 us
  starting transfers between devices: 11.2 us -> 0 us
    pallas_call x0 -> x2, Pallas kernels: none -> 196 us  [the longest x1 176 us: section(): pl.pallas_call(functools.partial(section_kernel, size, minor), in_specs=[...]
    all_to_all x2 -> x0, waiting for transfers between devices: 149 us -> none  [the longest x1 149 us: on_device(): lax.all_to_all(slab_spread(fields, group_size, slab_width, inverse_table)...]
    dot_general x7 -> x2, matrix products: 96.7 us -> 1.04 us  [the longest x1 0.65 us: back(): out = jnp.einsum('rflp,pk->rflk', rows, table, precision=high)]
    psum x1 -> x0, blocking collectives: 83.7 us -> none  [on_device(): summed = lax.psum(local_squares, ('py', 'pz'))]
    transpose x5 -> x2, local copies, waits for them, and re-layouts: 52.2 us -> 0.5 us  [the longest x1 0.46 us: ahead(): jnp.transpose(grid.reshape(2, 6, cross, group, chunks, TILE), (3, 4, 2, 0...]
    mul x14 -> x5, other arithmetic: 46.2 us -> 1.14 us  [the longest x4 1.06 us: projected(): return [keep * (field[i] - waves[i] * normal) for i in range(3)]]
    another operation x6 -> x1, local copies, waits for them, and re-layouts: 33.3 us -> 0.13 us  [__init__(): layer = velocity[:, :, 0, :].reshape(2, 3, cross, points)]
    reduce_max x1, other arithmetic: 17.2 us -> 0.61 us  [back(): fastest, squares = (jnp.max(numbers[:, 0]), jnp.sum(numbers[:, 1]))]
  transfers between devices with their start and end apart: 2 -> 0, of which waited for: 1 -> 0; matrix products, arithmetic and copies ran while one was open for 6% -> 0% of each run, Pallas kernels for 0% -> 0%
where the time goes in v1:
time: 222 us; the launch traced here: 219 us
  Pallas kernels  196 us (88%)
  local copies, waits for them, and re-layouts  8.62 us (4%)
  between operations  7.11 us (3%)
  other arithmetic  6.32 us (3%)
    pallas_call x1, Pallas kernels, section(): pl.pallas_call(functools.partial(section_kernel, size, minor), in_specs=[...  176 us
    pallas_call x1, Pallas kernels, close(): pl.pallas_call(functools.partial(close_kernel, size), grid_spec=pltpu.Pre...  20 us

profile of v1, /device:TPU:0, one launch (start us, length us, event | category | flops | bytes accessed | tf_op | source)
XLA Modules:
  0.0 219.1 jit_solution(4603273831522616142)
XLA Ops:
  0.6 0.0 copy-start.1
  1.9 1.3 pad_add_fusion.place_ref
  3.3 1.4 fusion.24
  5.3 0.7 abs_compare_fusion
  5.9 1.3 broadcast_compare_fusion
  7.3 0.1 convert_compare_fusion
  7.3 0.0 copy-start
  7.4 1.3 slice.182
  8.6 0.1 copy.37
  8.7 0.1 reshape_squeeze.3
  8.8 0.1 rev.6
  8.9 0.8 subtract_select_fusion.8
  9.7 0.1 subtract_select_fusion.7
  9.8 0.0 copy-done.1
  9.9 0.1 broadcast_multiply_fusion
  10.0 0.0 copy-done
  10.0 0.4 fusion
  10.4 0.1 slice_subtract_fusion
  10.6 0.2 copy.47
  10.8 0.2 copy.48
  11.0 0.1 maximum_bitcast_fusion
  11.1 0.5 copy.49
  11.6 0.6 reshape.1469
  12.2 0.9 copy.59.e_ref
  13.1 0.0 copy-start.2
  13.1 176.0 %section.1 = (f32[3,8,3,192,128]{4,3,2,1,0:T(8,128)}, f32[8,80,128]{2,1,0:T(8,128)}) custom-call(s32[3]{0:T(128)} %cut_ref.1, f32[8,72,128]{2,1,0:T(8,128)} %copy.59.e_ref, f32[2,3,96,4608]{3,2,1,0:T(8,128)} %v_ref.3, bf16[3,2,256,256]{3,2,1,0:T(8,128)(2,1)} %constant.91.clone.top_ref, bf16[3,2,256,256]{3,2,1,0:T(8,128)(2,1)} %constant.92.clone.rest_ref, ...), custom_call_target="tpu_custom_call" | custom-call | flops 49999998976 | bytes 40000000 | tf_op jit(solution)/shard_map/section/pallas_call | solution.py:566
  189.1 0.8 slice.202
  189.9 1.0 slice.204
  190.9 0.1 copy.51
  191.0 0.6 slice_reduce_fusion
  193.6 0.6 pad_maximum_fusion.1.scalar_ref
  194.2 0.0 copy-done.2
  194.2 0.1 multiply_add_fusion
  194.2 0.4 reshape.1471
  194.6 0.2 copy.65
  194.9 0.7 fusion.25
  195.5 0.1 slice_add_fusion.1
  195.6 0.1 subtract_select_fusion.5
  195.7 0.1 subtract_select_fusion.4
  195.9 0.1 rev.7
  196.0 0.1 broadcast_select_fusion
  196.1 0.8 reshape.1474.first_ref
  196.8 20.0 %close.1 = f32[2,3,96,4608]{3,2,1,0:T(8,128)} custom-call(s32[5]{0:T(128)} %pad_add_fusion.place_ref, f32[2]{0:T(128)} %pad_maximum_fusion.1.scalar_ref, f32[2,3,96,4608]{3,2,1,0:T(8,128)} %v_ref.3, f32[6,4608]{1,0:T(8,128)} %reshape.1474.first_ref, bf16[2,192,512]{2,1,0:T(8,128)(2,1)} %constant.101.clone.top_ref, ...), custom_call_target="tpu_custom_call" | custom-call | flops 5000000000 | bytes 40000000 | tf_op jit(solution)/shard_map/close/pallas_call | solution.py:609
  (15 shorter events, 0.2 us)
Async XLA Ops:
  0.6 9.2 %copy-start.1 = (f32[192]{0:T(256)S(1)}, f32[192]{0:T(256)}, u32[]{:S(2)}) copy-start(f32[192]{0:T(256)} %constant.110) | copy-start | bytes 2308
  7.3 2.7 %copy-start = (f32[192,384,1,1]{1,0,3,2:T(8,128)S(1)}, f32[192,384,1,1]{1,0,3,2:T(8,128)}, u32[]{:S(2)}) copy-start(f32[192,384,1,1]{1,0,3,2:T(8,128)} %constant.112) | copy-start | bytes 884740
  13.1 181.0 %copy-start.2 = (f32[192]{0:T(256)S(1)}, f32[192]{0:T(256)}, u32[]{:S(2)}) copy-start(f32[192]{0:T(256)} %constant.111) | copy-start | bytes 2308

commit v2 on v1

--- a/solution.py
+++ b/solution.py
@@ -73,18 +73,18 @@
             live = (index >= 0) & (index < self.points) & (np.abs(wave) <= self.limit)
             live = live[None, :] & (planes >= 0)[:, None]
             angle = 2.0 * np.pi * ((planes[:, None] * wave[None, :]) % self.points) / self.points
-            both.append((live * np.cos(angle), live * np.sin(angle), live * wave[None, :]))
+            both.append((live * np.cos(angle), live * np.sin(angle)))
         return both
 
     def spread_table(self, chunk):
         tables = []
-        for cosine, sine, wave in self.windows(self.planes_of(chunk).reshape(-1)):
-            tables.append(np.concatenate([cosine, sine, -wave * sine, wave * cosine]))
+        for cosine, sine in self.windows(self.planes_of(chunk).reshape(-1)):
+            tables.append(np.concatenate([cosine, sine]))
         return halves(np.stack(tables))
 
     def close_table(self):
         planes = np.stack([self.planes_of(c) for c in range(self.chunks)], axis=1).reshape(-1)
-        return halves(np.stack([np.concatenate([c, s], axis=1) for c, s, _ in self.windows(planes)]))
+        return halves(np.stack([np.concatenate([c, s], axis=1) for c, s in self.windows(planes)]))
 
     def angle(self, rows, cols):
         return 2.0 * np.pi * (np.outer(rows, cols) % self.points) / self.points
@@ -146,29 +146,34 @@
     return [keep * (field[i] - waves[i] * normal) for i in range(3)]
 
 
-def spread_pair(size, first_cross, mirrored, cutoffs, fields, top_ref, rest_ref, o_ref, base_row):
+def keep_pair(size, first_cross, cutoffs, fields, w_ref):
     waves, square, keep = pair_waves(size, first_cross, cutoffs)
     parts = [projected(waves, square, keep, fields[r]) for r in range(2)]
     whole = [jnp.concatenate([parts[0][i], parts[1][i]], axis=0) for i in range(3)]
-    tops, rests = zip(*[split(w) for w in whole])
+    along = waves[0]
+    for i in (1, 2):
+        whole.append(jnp.concatenate([-along * parts[1][i], along * parts[0][i]], axis=0))
+    for i in range(5):
+        top, rest = split(whole[i])
+        w_ref[0, i] = top
+        w_ref[1, i] = rest
+
+
+def spread_pair(size, mirrored, w_ref, top_ref, rest_ref, o_ref, base_row):
+    tops = [w_ref[0, i] for i in range(5)]
+    rests = [w_ref[1, i] for i in range(5)]
     count = size.group * TILE
     for which, begin in enumerate((0, size.start)):
         lanes = slice(begin, begin + size.window)
         top, rest = top_ref[which], rest_ref[which]
-        x_top, x_rest = tops[0][:, lanes], rests[0][:, lanes]
-        ahead = dot_rows(top[: 2 * count], x_top) + dot_rows(top[: 2 * count], x_rest)
-        ahead = ahead + dot_rows(rest[: 2 * count], x_top)
-        o_top = jnp.concatenate([tops[1][:, lanes], tops[2][:, lanes]], axis=0)
-        o_rest = jnp.concatenate([rests[1][:, lanes], rests[2][:, lanes]], axis=0)
-        other = dot_rows(top, o_top) + dot_rows(top, o_rest) + dot_rows(rest, o_top)
-        results = [ahead[:count] + turn(ahead[count:])]
-        for base in (0, 2 * count):
-            for i in range(2):
+        results = []
+        for fields in ((0,), (1, 2), (3, 4)):
+            w_top = jnp.concatenate([tops[i][:, lanes] for i in fields], axis=0)
+            w_rest = jnp.concatenate([rests[i][:, lanes] for i in fields], axis=0)
+            out = dot_rows(top, w_top) + dot_rows(top, w_rest) + dot_rows(rest, w_top)
+            for i in range(len(fields)):
                 cols = slice(i * LANES, (i + 1) * LANES)
-                results.append(
-                    other[base : base + count, cols]
-                    + turn(other[base + count : base + 2 * count, cols])
-                )
+                results.append(out[:count, cols] + turn(out[count:, cols]))
         slot = which + mirrored - 2 * which * mirrored
         at = pl.ds(pl.multiple_of(base_row + slot * TILE, TILE), TILE)
         for g in range(size.group):
@@ -285,9 +290,9 @@
 
 
 def section_kernel(size, minor, cut_ref, e_ref, v_ref, top_ref, rest_ref, ya, yb, yc, yd, za, zb, zc, zd,
-                   out_ref, last_ref, v_buf, send, recv, e_recv, back, last, sums, stats,
+                   out_ref, last_ref, place_ref, v_buf, send, recv, e_recv, back, last, sums, stats,
                    above, below, back_above, back_below, v_sem, e_sems, go_sems, come_sems,
-                   back_go, back_come, last_go, last_come, own_sems):
+                   back_go, back_come, last_go, last_come, own_sems, halves_buf):
     group, cross, chunks, limit = size.group, size.cross, size.chunks, size.limit
     steps = cross // 2
     me = lax.axis_index("py") * minor + lax.axis_index("pz")
@@ -302,6 +307,10 @@
         return (jnp.clip(kept, 0, cross) + 1) // 2
 
     mine = pairs_at(me)
+    place_ref[0] = me * cross
+    place_ref[1] = mirrored
+    for i in range(3):
+        place_ref[2 + i] = cut_ref[i]
     cutoffs = (cut_ref[0], cut_ref[1], cut_ref[2])
     cross_refs, depth_refs = (ya, yb, yc, yd), (za, zb, zc, zd)
     scratch = (above, below, back_above, back_below)
@@ -354,18 +363,21 @@
 
         @pl.when(p < mine)
         def _():
-            slot = (chunk * mine + p) % 2
-            fetch(p, slot).wait()
-            following = jnp.where(p + 1 < mine, p + 1, 0)
-
-            @pl.when((p + 1 < mine) | (chunk + 1 < chunks))
+            @pl.when(chunk == 0)
             def _():
-                fetch(following, 1 - slot).start()
-
-            j = p + mirrored * (steps - 1 - 2 * p)
-            fields = [[v_buf[slot, r, i, 1 : limit + 1, :] for i in range(3)] for r in range(2)]
+                slot = p % 2
+                fetch(p, slot).wait()
+
+                @pl.when(p + 1 < mine)
+                def _():
+                    fetch(p + 1, 1 - slot).start()
+
+                j = p + mirrored * (steps - 1 - 2 * p)
+                fields = [[v_buf[slot, r, i, 1 : limit + 1, :] for i in range(3)] for r in range(2)]
+                keep_pair(size, me * cross + 2 * j, cutoffs, fields, halves_buf.at[p])
+
             spread_pair(
-                size, me * cross + 2 * j, mirrored, cutoffs, fields,
+                size, mirrored, halves_buf.at[p],
                 top_ref.at[chunk], rest_ref.at[chunk], send.at[chunk], p * 2 * TILE,
             )
             rows = pl.ds(pl.multiple_of(p * 2 * TILE, 2 * TILE), 2 * TILE)
@@ -374,9 +386,7 @@
                     send.at[chunk, device, :, rows, :], recv.at[chunk, me, :, rows, :],
                     go_sems.at[chunk, off], come_sems.at[chunk, me], device,
                 ).start()
-            pltpu.make_async_copy(
-                send.at[chunk, me, :, rows, :], recv.at[chunk, me, :, rows, :], come_sems.at[chunk, me]
-            ).start()
+            recv[chunk, me, :, rows, :] = send[chunk, me, :, rows, :]
 
         return carry
 
@@ -389,7 +399,7 @@
     def middle_chunk(chunk, carry):
         for g in range(group):
             if counts[g]:
-                come_wait(chunk, g)
+                pl.when(me != g)(lambda g=g: come_wait(chunk, g))
 
         @pl.when(chunk == 0)
         def _():
@@ -493,9 +503,34 @@
     lax.fori_loop(0, chunks, back_sent, 0)
 
 
-def close_kernel(size, place_ref, scalar_ref, v_ref, first_ref, top_ref, rest_ref, *refs):
-    r_ref, o_ref = refs
-    step = pl.program_id(0)
+def close_kernel(size, place_ref, scalar_ref, first_ref, top_ref, rest_ref, *refs):
+    v_refs, refs = refs[:6], refs[6:]
+    r_refs, (out_ref, o_buf, o_sem) = refs[: size.chunks], refs[size.chunks :]
+    step, steps = pl.program_id(0), pl.num_programs(0)
+    buffer = step % 2
+    o_ref = o_buf.at[buffer]
+
+    def leave(at, slot):
+        lanes = pl.ds(pl.multiple_of(at * size.pair, LANES), size.pair)
+        return [
+            pltpu.make_async_copy(
+                o_buf.at[slot, r, i], out_ref.at[r, i, :, lanes], o_sem.at[slot, 3 * r + i]
+            )
+            for r in range(2)
+            for i in range(3)
+        ]
+
+    @pl.when(step < 2)
+    def _():
+        o_ref[:, :, size.limit + 1 :, :] = jnp.zeros(
+            (2, 3, o_buf.shape[3] - size.limit - 1, size.pair), f32
+        )
+
+    @pl.when(step >= 2)
+    def _():
+        for copy in leave(step - 2, buffer):
+            copy.wait()
+
     limit = size.limit
     results = [[[], []], [[], []], [[], []]]
     for which in range(2):
@@ -503,7 +538,7 @@
         at = pl.ds(pl.multiple_of(slot * TILE, TILE), TILE)
         for i in range(3):
             rows = jnp.concatenate(
-                [r_ref[c, g, i, at, :] for g in range(size.group) for c in range(size.chunks)], axis=0
+                [r[0, g, i, at, :] for g in range(size.group) for r in r_refs], axis=0
             )
             top, rest = split(rows.T)
             out = dot(top, top_ref[which]) + dot(top, rest_ref[which]) + dot(rest, top_ref[which])
@@ -525,16 +560,23 @@
     )
     forcing, step_size = scalar_ref[0], scalar_ref[1]
     gain = 1.0 + step_size * (forcing - viscosity * square)
-    depth = o_ref.shape[2]
     for r in range(2):
         solenoidal = projected(
-            waves, square, keep, [v_ref[r, i, 1 : limit + 1, :] for i in range(3)]
+            waves, square, keep, [v_refs[3 * r + i][0, 0, 1 : limit + 1, :] for i in range(3)]
         )
         forced = projected(waves, square, keep, [joined(*results[i][r]) for i in range(3)])
         for i in range(3):
             o_ref[r, i, 0:1, :] = first_ref[r * 3 + i : r * 3 + i + 1, :]
             o_ref[r, i, 1 : limit + 1, :] = solenoidal[i] * gain + jnp.where(keep > 0.0, step_size * forced[i], 0.0)
-            o_ref[r, i, limit + 1 :, :] = jnp.zeros((depth - limit - 1, size.pair), f32)
+
+
+    for copy in leave(step, buffer):
+        copy.start()
+
+    @pl.when(step == steps - 1)
+    def _():
+        for copy in leave(step - 1, 1 - buffer) + leave(step, buffer):
+            copy.wait()
 
 
 def whole_block(array):
@@ -566,10 +608,11 @@
     return pl.pallas_call(
         functools.partial(section_kernel, size, minor),
         in_specs=[pl.BlockSpec(memory_space=pltpu.SMEM), vmem, anywhere] + [vmem] * len(tables),
-        out_specs=[anywhere, anywhere],
+        out_specs=[anywhere, anywhere, pl.BlockSpec(memory_space=pltpu.SMEM)],
         out_shape=[
             jax.ShapeDtypeStruct((chunks, group, 3, size.rows, LANES), f32),
             jax.ShapeDtypeStruct((group, last_rows, LANES), f32),
+            jax.ShapeDtypeStruct((5,), jnp.int32),
         ],
         scratch_shapes=[
             pltpu.VMEM((2, 2, 3, kept_rows, size.pair), f32),
@@ -593,6 +636,7 @@
             dma((group,)),
             dma((group,)),
             dma((2,)),
+            pltpu.VMEM((cross // 2, 2, 5, LANES, size.pair), bf16),
         ],
         compiler_params=pltpu.CompilerParams(
             collective_id=0, has_side_effects=True, vmem_limit_bytes=60 * 1024 * 1024
@@ -605,7 +649,17 @@
 def close(size, place, scalars, velocity, first, returned):
     top, rest = (jnp.asarray(t) for t in size.close_table())
     steps = size.cross // 2
-    block = (2, 3, velocity.shape[2], size.pair)
+    kept_rows = -(-(size.limit + 1) // TILE) * TILE
+
+    def part(r, i):
+        return pl.BlockSpec((1, 1, kept_rows, size.pair), lambda j, p: (r, i, 0, j))
+
+    def chunk_block(c):
+        return pl.BlockSpec(
+            (1, size.group, 3, 2 * TILE, LANES),
+            lambda j, p: (c, 0, 0, jnp.where(p[1] == 1, steps - 1 - j, j), 0),
+        )
+
     return pl.pallas_call(
         functools.partial(close_kernel, size),
         grid_spec=pltpu.PrefetchScalarGridSpec(
@@ -613,22 +667,23 @@
             grid=(steps,),
             in_specs=[
                 pl.BlockSpec(memory_space=pltpu.SMEM),
-                pl.BlockSpec((2, 3, -(-(size.limit + 1) // TILE) * TILE, size.pair), lambda j, p: (0, 0, 0, j)),
                 pl.BlockSpec((6, size.pair), lambda j, p: (0, j)),
                 whole_block(top),
                 whole_block(rest),
-                pl.BlockSpec(
-                    (size.chunks, size.group, 3, 2 * TILE, LANES),
-                    lambda j, p: (0, 0, 0, jnp.where(p[1] == 1, steps - 1 - j, j), 0),
-                ),
+                *[part(r, i) for r in range(2) for i in range(3)],
+                *[chunk_block(c) for c in range(size.chunks)],
             ],
-            out_specs=pl.BlockSpec(block, lambda j, p: (0, 0, 0, j)),
+            out_specs=pl.BlockSpec(memory_space=pl.ANY),
+            scratch_shapes=[
+                pltpu.VMEM((2, 2, 3, velocity.shape[2], size.pair), f32),
+                pltpu.SemaphoreType.DMA((2, 6)),
+            ],
         ),
         out_shape=jax.ShapeDtypeStruct(velocity.shape, f32),
         compiler_params=params(),
         cost_estimate=cost(5e9, 4e7),
         name="close",
-    )(place, scalars, velocity, first, top, rest, returned)
+    )(place, scalars, first, top, rest, *[velocity] * 6, *[returned] * size.chunks)
 
 
 class Shallow:
@@ -643,7 +698,8 @@
         index = device * cross + jnp.where(mirrored, cross - 1 - spot, spot)
         self.mirrored = mirrored
         across = jnp.where(index < points // 2, index, index - points)
-        keep = (jnp.abs(along) <= cutoffs[0]) & (jnp.abs(across) <= cutoffs[1]) & (cutoffs[2] >= 0)
+        bounds = cutoffs.reshape(3, 1)
+        keep = (jnp.abs(along) <= bounds[0:1]) & (jnp.abs(across) <= bounds[1:2]) & (bounds[2:3] >= 0)
         self.keep = keep.astype(f32)
         self.waves = (along.astype(f32), across.astype(f32), jnp.zeros((1, 1), f32))
         self.square = self.waves[0] ** 2 + self.waves[1] ** 2
@@ -703,11 +759,8 @@
     points = 2 * velocity.shape[2]
     size = Sizes(points, group, velocity.shape[3] // points)
     device = lax.axis_index(GROUP)
-    place = jnp.stack(
-        [device * size.cross, (device >= group // 2).astype(jnp.int32), cutoffs[0], cutoffs[1], cutoffs[2]]
-    ).astype(jnp.int32)
     shallow = Shallow(size, velocity, cutoffs, device)
-    returned, got = section(size, lax.axis_size("pz"), cutoffs, shallow.ahead(), velocity)
+    returned, got, place = section(size, lax.axis_size("pz"), cutoffs, shallow.ahead(), velocity)
     forced, fastest, squares = shallow.back(got)
     step_size = time_step[0]
     energy = 0.5 * squares / float(points**3)

time: 222 us -> 219 us (0.986)
  no operation moved by 1% of the time
where the time goes in v2:
time: 219 us; the launch traced here: 218 us
  Pallas kernels  196 us (89%)
  local copies, waits for them, and re-layouts  8.6 us (4%)
  between operations  7.12 us (3%)
  other arithmetic  5.03 us (2%)
    pallas_call x1, Pallas kernels, section(): pl.pallas_call(functools.partial(section_kernel, size, minor), in_specs=[...  176 us
    pallas_call x1, Pallas kernels, close(): pl.pallas_call(functools.partial(close_kernel, size), grid_spec=pltpu.Pre...  20.1 us

profile of v2, /device:TPU:0, one launch (start us, length us, event | category | flops | bytes accessed | tf_op | source)
XLA Modules:
  0.0 218.2 jit_solution(7195544092020625477)
XLA Ops:
  0.6 0.0 copy-start.1
  2.0 1.4 fusion.24
  4.0 0.7 abs_compare_fusion
  4.6 1.3 broadcast_compare_fusion
  6.0 0.1 convert_compare_fusion
  6.0 0.0 copy-start
  6.1 1.3 slice.181
  7.3 0.1 copy.37
  7.4 0.1 reshape_squeeze.3
  7.5 0.1 rev.6
  7.6 0.8 subtract_select_fusion.8
  8.4 0.1 subtract_select_fusion.7
  8.5 0.0 copy-done.1
  8.6 0.1 broadcast_multiply_fusion
  8.7 0.0 copy-done
  8.7 0.4 fusion
  9.1 0.1 slice_subtract_fusion
  9.3 0.2 copy.47
  9.5 0.2 copy.48
  9.7 0.1 maximum_bitcast_fusion
  9.8 0.5 copy.49
  10.3 0.6 reshape.1480
  10.9 0.9 copy.59.e_ref
  11.8 0.0 copy-start.2
  11.8 176.3 %section.1 = (f32[3,8,3,192,128]{4,3,2,1,0:T(8,128)}, f32[8,80,128]{2,1,0:T(8,128)}, s32[5]{0:T(128)}) custom-call(s32[3]{0:T(128)} %cut_ref.1, f32[8,72,128]{2,1,0:T(8,128)} %copy.59.e_ref, f32[2,3,96,4608]{3,2,1,0:T(8,128)} %refs_5_.1, bf16[3,2,128,256]{3,2,1,0:T(8,128)(2,1)} %constant.92.clone.top_ref, bf16[3,2,128,256]{3,2,1,0:T(8,128)(2,1)} %constant.93.clone.rest_ref, ...), custom_call_target="tpu_custom_call" | custom-call | flops 49999998976 | bytes 40000000 | tf_op jit(solution)/shard_map/section/pallas_call | solution.py:608
  188.2 0.8 slice.201
  188.9 1.0 slice.203
  189.9 0.1 copy.51
  190.0 0.6 slice_reduce_fusion
  192.6 0.6 pad_maximum_fusion.1.scalar_ref
  193.2 0.0 copy-done.2
  193.2 0.1 multiply_add_fusion
  193.3 0.4 reshape.1482
  193.6 0.2 copy.65
  193.9 0.7 fusion.25
  194.6 0.1 slice_add_fusion.1
  194.7 0.1 subtract_select_fusion.5
  194.8 0.1 subtract_select_fusion.4
  194.9 0.1 rev.7
  195.0 0.1 broadcast_select_fusion
  195.1 0.8 reshape.1485.first_ref
  195.9 20.1 %close.1 = f32[2,3,96,4608]{3,2,1,0:T(8,128)} custom-call(s32[5]{0:T(128)} %get-tuple-element.6.place_ref, f32[2]{0:T(128)} %pad_maximum_fusion.1.scalar_ref, f32[6,4608]{1,0:T(8,128)} %reshape.1485.first_ref, bf16[2,192,512]{2,1,0:T(8,128)(2,1)} %constant.102.clone.top_ref, bf16[2,192,512]{2,1,0:T(8,128)(2,1)} %constant.103.clone.rest_ref, ...), custom_call_target="tpu_custom_call" | custom-call | flops 5000000000 | bytes 40000000 | tf_op jit(solution)/shard_map/close/pallas_call | solution.py:663
  (15 shorter events, 0.2 us)
Async XLA Ops:
  0.6 7.9 %copy-start.1 = (f32[192]{0:T(256)S(1)}, f32[192]{0:T(256)}, u32[]{:S(2)}) copy-start(f32[192]{0:T(256)} %constant.111) | copy-start | bytes 2308
  6.0 2.7 %copy-start = (f32[192,384,1,1]{1,0,3,2:T(8,128)S(1)}, f32[192,384,1,1]{1,0,3,2:T(8,128)}, u32[]{:S(2)}) copy-start(f32[192,384,1,1]{1,0,3,2:T(8,128)} %constant.113) | copy-start | bytes 884740
  11.8 181.4 %copy-start.2 = (f32[192]{0:T(256)S(1)}, f32[192]{0:T(256)}, u32[]{:S(2)}) copy-start(f32[192]{0:T(256)} %constant.112) | copy-start | bytes 2308
